TPU v7x, 128 devices: a whole 4x4x4 slice. The times are simulated.
128 devices in a mesh: group: 16 (over x, z_lo, core), head: 8 (over y, z_hi).
Axes of the slice: x: 4, y: 4, z: 4 (z_hi: 2, z_lo: 2; z = z_hi * 2 + z_lo), core: 2. Of those that a mesh axis runs over, the one named last changes fastest.
Arguments:
- hidden_in: bfloat16 [256, 2560], P('group'), may hold values from -6 to 6
- ssm_state: float32 [256, 80, 64, 128], P('group', 'head'), may hold values from -6 to 6
- conv_x_state: bfloat16 [256, 3, 5120], P('group', None, 'head'), may hold values from -6 to 6
- conv_bc_state: bfloat16 [256, 3, 256], P('group'), may hold values from -6 to 6
- token_ids: int32 [256], P('group'), may hold values from 0 to 25599
- ref_logits: bfloat16 [256, 25600], P('group', 'head'), may hold values from -15 to 350
- in_z: bfloat16 [2560, 5120], P('group', 'head'), may hold values from -0.125 to 0.125
- in_x: bfloat16 [2560, 5120], P('group', 'head'), may hold values from -0.125 to 0.125
- in_bc: bfloat16 [2560, 256], P('group'), may hold values from -0.125 to 0.125
- in_dt: bfloat16 [2560, 80], P('group', 'head'), may hold values from -0.125 to 0.125
- out_t: bfloat16 [2560, 5120], P('group', 'head'), may hold values from -0.078125 to 0.078125
- lm_head: bfloat16 [25600, 2560], P('head', 'group'), may hold values from -6 to 6
- conv_wx: float32 [4, 5120], P(None, 'head'), may hold values from -3 to 3
- conv_bx: float32 [5120], P('head'), may hold values from -1.5 to 1.5
- conv_wbc: float32 [4, 256], replicated, may hold values from -3 to 3
- conv_bbc: float32 [256], replicated, may hold values from -1.5 to 1.5
- dt_bias: float32 [80], P('head'), may hold values from -4 to -1
- a_log: float32 [80], P('head'), may hold values from 0 to 2.77
- skip_gain: float32 [80], P('head'), may hold values from 0.5 to 1.5
- norm_in: float32 [2560], replicated, may hold values from 0.5 to 1.5
- norm_gain: float32 [5120], P('head'), may hold values from 0.5 to 1.5
- final_gain: float32 [2560], replicated, may hold values from 0.5 to 1.5
Outputs:
- new_state: float32 [256, 80, 64, 128], P('group', 'head')
- divergence: float32 [256], P('group')
- token_logprob: float32 [256], P('group')
- roll_z: bfloat16 [2560, 5120], P(None, 'head')
- roll_x: bfloat16 [2560, 5120], P(None, 'head')
- roll_bc: bfloat16 [2560, 256], replicated
- roll_dt: bfloat16 [2560, 80], P(None, 'head')
- roll_out: bfloat16 [2560, 5120], P(None, 'head')
All inputs are finite; a program needn't handle non-finite values.
Results may differ from a plain program's by a relative error of at most 0.0102.
Values may be sent and summed in bfloat16 or wider, within the bound.
A program may use at most 128 MiB of HBM per device.

v0:
```python
import jax
import jax.numpy as jnp
from jax import lax
from jax.sharding import PartitionSpec as P

P_SIZE = 64
EPSILON = 1e-05


def sent_together(arrays, axis, dim, along):
    both = jnp.concatenate(arrays, axis=along)
    result, at, done = (lax.all_gather(both, axis, axis=dim, tiled=True), 0, [])
    for a in arrays:
        done.append(lax.slice_in_dim(result, at, at + a.shape[along], axis=along))
        at += a.shape[along]
    return tuple(done)


def from_everyone(array, axis):
    peers = lax.axis_size(axis)
    return lax.all_to_all(
        jnp.broadcast_to(array[None], (peers, *array.shape)), axis, 0, 0, tiled=True
    )


def taken_together(array, axis):
    everything = from_everyone(array, axis)
    return jnp.sum(everything, axis=0)


def collected_together(array, axis):
    leaves = jax.tree.leaves(array)
    sequence = sorted(range(len(leaves)), key=lambda k: -leaves[k].size)
    width = (1, *leaves[sequence[0]].shape)[-1]
    lines = [
        jnp.pad(leaves[k].reshape(-1), (0, -leaves[k].size % width)).reshape(-1, width)
        for k in sequence
    ]
    both, at, found = (from_everyone(jnp.concatenate(lines), axis), 0, {})
    for k, line in zip(sequence, lines):
        piece = both[:, at : at + len(line)].reshape(len(both), -1)
        found[k] = piece[:, : leaves[k].size].reshape(-1, *leaves[k].shape)
        at += len(line)
    numbers = iter(range(len(leaves)))
    return jax.tree.map(lambda _: found[next(numbers)], array)


def folded_in_pairs(pieces, combine):
    while len(jax.tree.leaves(pieces)[0]) > 1:
        pieces = jax.vmap(combine)(
            *(jax.tree.map(lambda part: part[side::2], pieces) for side in (0, 1))
        )
    return jax.tree.map(lambda part: part[0], pieces)


def combined_all(array, axis, combine):
    pieces = collected_together(array, axis)
    return folded_in_pairs(pieces, combine)


def rms_norm(values, gain):
    return values * lax.rsqrt(jnp.mean(values * values, axis=-1, keepdims=True) + EPSILON) * gain


def causal_conv(history, newest, taps, offset):
    window = jnp.concatenate([history, newest[:, None, :]], axis=1).astype(jnp.float32)
    return jax.nn.silu(jnp.sum(window * taps[None, :, :], axis=1) + offset)


def combine_stats(first, second):
    roll_max = jnp.maximum(first[0], second[0])
    roll_sum = first[1] * jnp.exp(first[0] - roll_max) + second[1] * jnp.exp(second[0] - roll_max)
    ref_max = jnp.maximum(first[2], second[2])
    scale_first = jnp.exp(first[2] - ref_max)
    scale_second = jnp.exp(second[2] - ref_max)
    ref_sum = first[3] * scale_first + second[3] * scale_second
    cross_sum = first[4] * scale_first + second[4] * scale_second
    return (roll_max, roll_sum, ref_max, ref_sum, cross_sum, first[5] + second[5])


def shards(
    hidden_in,
    ssm_state,
    conv_x_state,
    conv_bc_state,
    token_ids,
    ref_logits,
    in_z,
    in_x,
    in_bc,
    in_dt,
    out_t,
    lm_head,
    conv_wx,
    conv_bx,
    conv_wbc,
    conv_bbc,
    dt_bias,
    a_log,
    skip_gain,
    norm_in,
    norm_gain,
    final_gain,
):
    roll_z, roll_x, roll_bc, roll_dt, roll_out = sent_together(
        (in_z, in_x, in_bc, in_dt, out_t), "group", 0, 1
    )
    stream_in = hidden_in.astype(jnp.float32)
    normed = rms_norm(stream_in, norm_in).astype(jnp.bfloat16)
    gate_branch = jnp.dot(normed, roll_z, preferred_element_type=jnp.float32).astype(jnp.bfloat16)
    x_branch = jnp.dot(normed, roll_x, preferred_element_type=jnp.float32).astype(jnp.bfloat16)
    bc_branch = jnp.dot(normed, roll_bc, preferred_element_type=jnp.float32).astype(jnp.bfloat16)
    step_raw = jnp.dot(normed, roll_dt, preferred_element_type=jnp.float32).astype(jnp.bfloat16)
    x_conv = causal_conv(conv_x_state, x_branch, conv_wx, conv_bx)
    bc_conv = causal_conv(conv_bc_state, bc_branch, conv_wbc, conv_bbc)
    state_size = bc_conv.shape[1] // 2
    b_vals = bc_conv[:, :state_size]
    c_vals = bc_conv[:, state_size:]
    step = jax.nn.softplus(step_raw.astype(jnp.float32) + dt_bias)
    decay = jnp.exp(-step * jnp.exp(a_log))
    seq_count = x_conv.shape[0]
    local_heads = a_log.shape[0]
    x_heads = x_conv.reshape(seq_count, local_heads, P_SIZE)
    inflow = (step[:, :, None] * x_heads)[:, :, :, None] * b_vals[:, None, None, :]
    new_state = decay[:, :, None, None] * ssm_state + inflow
    ssm_out = jnp.einsum("shpn,sn->shp", new_state, c_vals)
    ssm_out = (ssm_out + skip_gain[None, :, None] * x_heads).reshape(
        seq_count, local_heads * P_SIZE
    )
    gated = ssm_out * jax.nn.silu(gate_branch.astype(jnp.float32))
    square_total = taken_together(jnp.sum(gated * gated, axis=-1), "head")
    inner_width = gated.shape[1] * lax.axis_size("head")
    gated_out = (
        gated * lax.rsqrt(square_total / inner_width + EPSILON)[:, None] * norm_gain
    ).astype(jnp.bfloat16)
    partial_mix = lax.dot_general(
        gated_out, roll_out, (((1,), (1,)), ((), ())), preferred_element_type=jnp.float32
    )
    mixed = taken_together(partial_mix, "head")
    final_hidden = rms_norm(stream_in + mixed, final_gain).astype(jnp.bfloat16)
    vocab_local = lm_head.shape[0]
    logits = lax.dot_general(
        final_hidden,
        lax.all_gather(lm_head, "group", axis=1, tiled=True),
        (((1,), (1,)), ((), ())),
        preferred_element_type=jnp.float32,
    )
    reference_rows = ref_logits.astype(jnp.float32)
    column_ids = lax.axis_index("head") * vocab_local + lax.broadcasted_iota(
        jnp.int32, (1, vocab_local), 1
    )
    picked_part = jnp.sum(jnp.where(column_ids == token_ids[:, None], logits, 0.0), axis=-1)
    roll_local = jnp.max(logits, axis=-1)
    ref_local = jnp.max(reference_rows, axis=-1)
    roll_sum = jnp.sum(jnp.exp(logits - roll_local[:, None]), axis=-1)
    ref_weights = jnp.exp(reference_rows - ref_local[:, None])
    ref_sum = jnp.sum(ref_weights, axis=-1)
    cross_sum = jnp.sum(ref_weights * (reference_rows - logits), axis=-1)
    roll_max, roll_sum, ref_max, ref_sum, cross_sum, picked = combined_all(
        (roll_local, roll_sum, ref_local, ref_sum, cross_sum, picked_part), "head", combine_stats
    )
    lse_roll = roll_max + jnp.log(roll_sum)
    lse_ref = ref_max + jnp.log(ref_sum)
    divergence = cross_sum / ref_sum - lse_ref + lse_roll
    token_logprob = picked - lse_roll
    return (new_state, divergence, token_logprob, roll_z, roll_x, roll_bc, roll_dt, roll_out)


def solution(mesh):
    return jax.shard_map(
        shards,
        mesh=mesh,
        in_specs=(
            P("group", None),
            P("group", "head", None, None),
            P("group", None, "head"),
            P("group", None, None),
            P("group"),
            P("group", "head"),
            P("group", "head"),
            P("group", "head"),
            P("group", None),
            P("group", "head"),
            P("group", "head"),
            P("head", "group"),
            P(None, "head"),
            P("head"),
            P(),
            P(),
            P("head"),
            P("head"),
            P("head"),
            P(),
            P("head"),
            P(),
        ),
        out_specs=(
            P("group", "head", None, None),
            P("group"),
            P("group"),
            P(None, "head"),
            P(None, "head"),
            P(),
            P(None, "head"),
            P(None, "head"),
        ),
        check_vma=False,
    )
```

profile of v0, /device:TPU:0, one launch (start us, length us, event | category | flops | bytes accessed | tf_op | source)
XLA Modules:
  0.0 219.2 jit_solution(8908940668585763981)
XLA Ops:
  7.2 0.0 copy-start.16
  7.2 0.0 copy-start.12
  7.2 0.0 copy-start.4
  7.2 0.0 all-gather.3.cloned.1.call-start
  7.2 0.8 copy.50
  8.1 2.1 concatenate.12
  10.1 0.0 all-gather.3.cloned.1.call-update
  10.2 0.0 all-gather.5.cloned.1.call-start
  10.2 0.7 all-gather.5.cloned.1.call-update
  10.9 0.0 copy-done.16
  10.9 0.5 exp.69
  11.4 0.0 copy-done.12
  11.4 0.1 add.148
  11.5 0.0 copy-done.4
  11.5 0.1 fusion.9
  11.7 69.3 %all-gather.3.cloned.1.call-done = bf16[2560,2186]{1,0:T(8,128)(2,1)} async-done(((bf16[160,2186]{1,0:T(8,128)(2,1)}), bf16[2560,2186]{1,0:T(8,128)(2,1)}) %all-gather.3.cloned.1.call-update) | async-done | bytes 11192336 | tf_op jit(solution)/shard_map/all_gather | solution.py:12
  81.0 6.3 %fusion.26 = (bf16[2560,640]{1,0:T(8,128)(2,1)S(1)}, bf16[2560,640]{1,0:T(8,128)(2,1)}, bf16[2560,640]{1,0:T(8,128)(2,1)S(1)}) fusion(bf16[2560,2186]{1,0:T(8,128)(2,1)} %all-gather.3.cloned.1.call-done), kind=kLoop, calls=%fused_computation.67 | loop fusion | bytes 19660800 | tf_op jit(solution)/shard_map/slice | solution.py:14
  87.3 0.0 copy-start.10
  87.3 1.7 copy-done.2
  89.0 0.0 copy-done.6
  89.0 0.6 fusion.1
  89.5 0.0 copy-done.7
  89.5 0.0 copy-done.10
  89.6 0.1 reduce_sum.103
  89.7 0.0 copy-start.9
  89.7 0.0 copy-start.13
  89.7 1.4 slice.210
  91.1 0.0 copy-start.3
  91.1 0.3 fusion.2
  91.4 0.0 copy-done.9
  91.4 0.0 copy-done.13
  91.5 0.7 divide_multiply_fusion.1
  92.2 1.6 multiply_exponential_fusion
  93.8 0.1 broadcast_multiply_fusion
  93.9 4.2 %multiply_add_fusion = f32[16,10,64,128]{3,2,1,0:T(8,128)S(1)} fusion(f32[16,10,64,128]{3,2,1,0:T(8,128)} %param.23, f32[16,128]{1,0:T(8,128)S(1)} %get-tuple-element.72, f32[16,10,64]{2,1,0:T(8,128)S(1)} %broadcast_multiply_fusion, f32[16,10]{1,0:T(8,128)S(1)} %get-tuple-element.75), kind=kLoop, calls=%fused_computation | loop fusion | flops 3932160 | bytes 10535552 | tf_op jit(solution)/shard_map/add | solution.py:125
  98.1 0.0 copy-done.3
  98.1 0.0 copy-start
  98.1 0.0 copy-start.14
  98.1 2.3 %copy-done = f32[16,10,64,128]{3,2,1,0:T(8,128)} copy-done((f32[16,10,64,128]{3,2,1,0:T(8,128)}, f32[16,10,64,128]{3,2,1,0:T(8,128)S(1)}, u32[]{:S(2)}) %copy-start) | copy-done | bytes 5242904
  100.5 2.1 fusion.30
  102.6 0.0 copy-done.14
  102.6 0.7 bitcast_add_fusion
  103.3 1.0 reshape.143
  104.3 0.7 multiply_reduce_fusion.3
  105.0 14.1 %all_to_all.16 = f32[8,1,16]{2,1,0:T(1,128)S(1)} all-to-all(f32[8,1,16]{2,1,0:T(1,128)S(1)} %broadcast_in_dim.15), channel_id=1, replica_groups=mesh['group'=16,'head'=8] {'head'}, dimensions={0} | all-to-all | bytes 1024 | tf_op jit(solution)/shard_map/all_to_all | solution.py:21
  119.2 0.0 copy-start.5
  119.2 3.0 %fusion.15 = f32[16,2560]{1,0:T(8,128)S(1)} fusion(bf16[2560,640]{1,0:T(8,128)(2,1)} %get-tuple-element.63, f32[16,640]{1,0:T(8,128)S(1)} %get-tuple-element.78, f32[640]{0:T(1024)S(1)} %copy-done.11, f32[16]{0:T(128)S(1)} %add_rsqrt_fusion.1), kind=kOutput, calls=%fused_computation.38 | convolution fusion | flops 52459520 | bytes 3484224 | tf_op jit(solution)/shard_map/dot_general | solution.py:136
  122.2 1.2 broadcast_in_dim.16
  123.5 3.6 %all-to-all-start.1 = ((f32[8,16,2560]{2,1,0:T(8,128)}), f32[8,16,2560]{2,1,0:T(8,128)S(1)}, u32[]{:S(2)}, u32[]{:S(2)}) async-start(f32[8,16,2560]{2,1,0:T(8,128)} %broadcast_in_dim.16), calls=%async_computation.1 | async-start | bytes 2621440 | tf_op jit(solution)/shard_map/all_to_all | solution.py:21
  127.1 0.1 reduce_max.28
  127.2 21.8 %all-to-all-done.1 = f32[8,16,2560]{2,1,0:T(8,128)S(1)} async-done(((f32[8,16,2560]{2,1,0:T(8,128)}), f32[8,16,2560]{2,1,0:T(8,128)S(1)}, u32[]{:S(2)}, u32[]{:S(2)}) %all-to-all-start.1) | async-done | bytes 1310752 | tf_op jit(solution)/shard_map/all_to_all | solution.py:21
  149.1 0.1 reduce_sum.107
  149.1 0.1 multiply_reduce_fusion
  149.3 0.0 slice-start
  149.3 38.0 %all-gather.5.cloned.1.call-done = bf16[3200,2560]{0,1:T(8,128)(2,1)} async-done(((bf16[3200,160]{0,1:T(8,128)(2,1)}), bf16[3200,2560]{0,1:T(8,128)(2,1)}) %all-gather.5.cloned.1.call-update) | async-done | bytes 16384016 | tf_op jit(solution)/shard_map/all_gather | solution.py:144
  187.3 0.0 copy-done.8
  187.3 8.0 %fusion.29 = (f32[16]{0:T(128)S(1)}, f32[16,3200]{1,0:T(8,128)S(1)}) fusion(bf16[3200,2560]{0,1:T(8,128)(2,1)} %all-gather.5.cloned.1.call-done, f32[16,2560]{1,0:T(8,128)S(1)} %reduce_sum.107, bf16[16,2560]{1,0:T(8,128)(2,1)S(1)} %copy-done.4, f32[2560]{0:T(1024)S(1)} %copy-done.8, f32[16]{0:T(128)S(1)} %add_rsqrt_fusion), kind=kOutput, calls=%fused_computation.70 | convolution fusion | flops 262399984 | bytes 16844928 | tf_op jit(solution)/shard_map/dot_general | solution.py:142
  195.4 0.3 select_reduce_fusion
  195.7 0.6 broadcast_in_dim.18
  196.3 6.6 %all-to-all-start.2 = ((f32[8,6,16]{2,1,0:T(8,128)}), f32[8,6,16]{2,1,0:T(8,128)S(1)}, u32[]{:S(2)}, u32[]{:S(2)}) async-start(f32[8,6,16]{2,1,0:T(8,128)} %broadcast_in_dim.18), calls=%async_computation.2 | async-start | bytes 65536 | tf_op jit(solution)/shard_map/all_to_all | solution.py:21
  202.9 0.9 copy.58
  203.8 6.8 %all-to-all-done.2 = f32[8,6,16]{2,1,0:T(8,128)S(1)} async-done(((f32[8,6,16]{2,1,0:T(8,128)}), f32[8,6,16]{2,1,0:T(8,128)S(1)}, u32[]{:S(2)}, u32[]{:S(2)}) %all-to-all-start.2) | async-done | bytes 3104 | tf_op jit(solution)/shard_map/all_to_all | solution.py:21
  211.3 0.5 subtract_bitcast_fusion
  211.9 0.5 add_bitcast_fusion
  (56 shorter events, 0.8 us)
Async XLA Ops:
  7.2 3.7 %copy-start.16 = (f32[10]{0:T(128)S(1)}, f32[10]{0:T(128)}, u32[]{:S(2)}) copy-start(f32[10]{0:T(128)} %param.39) | copy-start | bytes 124
  7.2 4.3 %copy-start.12 = (f32[640]{0:T(1024)S(1)}, f32[640]{0:T(1024)}, u32[]{:S(2)}) copy-start(f32[640]{0:T(1024)} %param.35) | copy-start | bytes 7684
  7.2 4.3 %copy-start.4 = (bf16[16,2560]{1,0:T(8,128)(2,1)S(1)}, bf16[16,2560]{1,0:T(8,128)(2,1)}, u32[]{:S(2)}) copy-start(bf16[16,2560]{1,0:T(8,128)(2,1)} %param.22) | copy-start | bytes 245764
  7.2 73.8 %all-gather.3.cloned.1.call-start = ((), (), s32[]{:S(2)}) async-start(), calls=%async_computation.3 | async-start | bytes 12533760 | tf_op jit(solution)/shard_map/all_gather | solution.py:12
  10.2 177.2 %all-gather.5.cloned.1.call-start = ((), (), s32[]{:S(2)}) async-start(), calls=%async_computation.4 | async-start | bytes 17408000 | tf_op jit(solution)/shard_map/all_gather | solution.py:144
  11.7 77.3 %copy-start.6 = (f32[2560]{0:T(1024)S(1)}, f32[2560]{0:T(1024)}, u32[]{:S(2)}) copy-start(f32[2560]{0:T(1024)} %param.41) | copy-start | bytes 30724
  87.3 1.7 copy-start.2
  87.3 17.1 %copy-start.1 = (bf16[2560,640]{1,0:T(8,128)(2,1)}, bf16[2560,640]{1,0:T(8,128)(2,1)S(1)}, u32[]{:S(2)}) copy-start(bf16[2560,640]{1,0:T(8,128)(2,1)S(1)} %get-tuple-element.62) | copy-start | bytes 9830404
  87.3 2.3 %copy-start.7 = (bf16[16,3,640]{2,0,1:T(8,128)(2,1)S(1)}, bf16[16,3,640]{2,0,1:T(8,128)(2,1)}, u32[]{:S(2)}) copy-start(bf16[16,3,640]{2,0,1:T(8,128)(2,1)} %param.24) | copy-start | bytes 184324
  87.3 2.3 %copy-start.10 = (f32[4,640]{1,0:T(4,128)S(1)}, f32[4,640]{1,0:T(4,128)}, u32[]{:S(2)}) copy-start(f32[4,640]{1,0:T(4,128)} %param.34) | copy-start | bytes 30724
  89.7 1.8 copy-start.9
  89.7 1.8 copy-start.13
  91.1 7.0 %copy-start.3 = (bf16[2560,256]{1,0:T(8,128)(2,1)}, bf16[2560,256]{1,0:T(8,128)(2,1)S(1)}, u32[]{:S(2)}) copy-start(bf16[2560,256]{1,0:T(8,128)(2,1)S(1)} %slice.210) | copy-start | bytes 3932164
  98.1 2.4 %copy-start = (f32[16,10,64,128]{3,2,1,0:T(8,128)}, f32[16,10,64,128]{3,2,1,0:T(8,128)S(1)}, u32[]{:S(2)}) copy-start(f32[16,10,64,128]{3,2,1,0:T(8,128)S(1)} %multiply_add_fusion) | copy-start | bytes 15728644
  98.1 4.5 %copy-start.14 = (f32[10]{0:T(128)S(1)}, f32[10]{0:T(128)}, u32[]{:S(2)}) copy-start(f32[10]{0:T(128)} %param.40) | copy-start | bytes 124
  102.6 16.6 %copy-start.11 = (f32[640]{0:T(1024)S(1)}, f32[640]{0:T(1024)}, u32[]{:S(2)}) copy-start(f32[640]{0:T(1024)} %param.42) | copy-start | bytes 7684
  119.2 7.8 %copy-start.5 = (bf16[16,3200]{1,0:T(8,128)(2,1)S(1)}, bf16[16,3200]{1,0:T(8,128)(2,1)}, u32[]{:S(2)}) copy-start(bf16[16,3200]{1,0:T(8,128)(2,1)} %param.27) | copy-start | bytes 307204
  122.2 65.1 %copy-start.8 = (f32[2560]{0:T(1024)S(1)}, f32[2560]{0:T(1024)}, u32[]{:S(2)}) copy-start(f32[2560]{0:T(1024)} %param.43) | copy-start | bytes 30724
  123.5 25.6 %all-to-all-start.1 = ((f32[8,16,2560]{2,1,0:T(8,128)}), f32[8,16,2560]{2,1,0:T(8,128)S(1)}, u32[]{:S(2)}, u32[]{:S(2)}) async-start(f32[8,16,2560]{2,1,0:T(8,128)} %broadcast_in_dim.16), calls=%async_computation.1 | async-start | bytes 2621440 | tf_op jit(solution)/shard_map/all_to_all | solution.py:21
  149.3 46.1 %copy-start.15 = (s32[16]{0:T(128)S(1)}, s32[16]{0:T(128)}, u32[]{:S(2)}) copy-start(s32[16]{0:T(128)} %param.26) | copy-start | bytes 196
  149.3 53.6 %slice-start = ((bf16[2560,2186]{1,0:T(8,128)(2,1)}), bf16[2560,10]{1,0:T(8,128)(2,1)S(1)}, s32[]{:S(2)}) async-start(bf16[2560,2186]{1,0:T(8,128)(2,1)} %all-gather.3.cloned.1.call-done), calls=%async_computation.5 | async-start | bytes 1310720 | tf_op jit(solution)/shard_map/slice | solution.py:14
  196.3 14.3 %all-to-all-start.2 = ((f32[8,6,16]{2,1,0:T(8,128)}), f32[8,6,16]{2,1,0:T(8,128)S(1)}, u32[]{:S(2)}, u32[]{:S(2)}) async-start(f32[8,6,16]{2,1,0:T(8,128)} %broadcast_in_dim.18), calls=%async_computation.2 | async-start | bytes 65536 | tf_op jit(solution)/shard_map/all_to_all | solution.py:21
Sparse Core Ops, SparseCore 0:
  10.3 70.6 all-gather.2
  82.7 104.5 all-gather.4
where the time goes:
time: 220 us; the launch traced here: 219 us
  waiting for transfers between devices  137 us (62%)
  local copies, waits for them, and re-layouts  19.7 us (9%)
  matrix products  16.4 us (7%)
  between operations  14.3 us (6%)
  blocking collectives  14.1 us (6%)
  starting transfers between devices  10.2 us (5%)
  other arithmetic  7.78 us (4%)
    all_gather x1, waiting for transfers between devices, sent_together(): result, at, done = (lax.all_gather(both, axis, axis=dim, tiled=True), 0, [])  69.3 us
    all_gather x1, waiting for transfers between devices, shards(): lax.all_gather(lm_head, 'group', axis=1, tiled=True)  38 us
    all_to_all x2, waiting for transfers between devices, from_everyone(): lax.all_to_all(jnp.broadcast_to(array[None], (peers, *array.shape)), axis...  28.6 us
    all_to_all x1, blocking collectives, from_everyone(): lax.all_to_all(jnp.broadcast_to(array[None], (peers, *array.shape)), axis...  14.1 us
    all_to_all x2, starting transfers between devices, from_everyone(): lax.all_to_all(jnp.broadcast_to(array[None], (peers, *array.shape)), axis...  10.2 us
    dot_general x1, matrix products, shards(): lax.dot_general(final_hidden, lax.all_gather(lm_head, 'group', axis=1, ti...  8.03 us
    slice x4, local copies, waits for them, and re-layouts, sent_together(): done.append(lax.slice_in_dim(result, at, at + a.shape[along], axis=along))  7.68 us
    unnamed x36, local copies, waits for them, and re-layouts  5.83 us
  transfers between devices with their start and end apart: 4, of which 4 were waited for; matrix products, arithmetic and copies ran while one was open for 12% of the time, Pallas kernels for 0%

commit v1 on v0

--- a/solution.py
+++ b/solution.py
@@ -5,6 +5,15 @@
 
 P_SIZE = 64
 EPSILON = 1e-05
+numbers_post = lambda local: jnp.concatenate(
+    lax.all_to_all(
+        jnp.stack([local for _ in range(lax.axis_size("group"))]),
+        "group",
+        split_axis=0,
+        concat_axis=0,
+    ),
+    axis=1,
+)
 
 
 def sent_together(arrays, axis, dim, along):
@@ -141,7 +150,7 @@
     vocab_local = lm_head.shape[0]
     logits = lax.dot_general(
         final_hidden,
-        lax.all_gather(lm_head, "group", axis=1, tiled=True),
+        numbers_post(lm_head),
         (((1,), (1,)), ((), ())),
         preferred_element_type=jnp.float32,
     )

time: 220 us -> 450 us (2.05)
  waiting for transfers between devices: 137 us -> 339 us
  blocking collectives: 14.1 us -> 35.6 us
  local copies, waits for them, and re-layouts: 19.7 us -> 26.3 us
    all_to_all x0 -> x1, waiting for transfers between devices: none -> 264 us  [lax.all_to_all(jnp.stack([local for _ in range(lax.axis_size('group'))]),...]
    all_gather x1 -> x0, waiting for transfers between devices: 38 us -> none  [shards(): lax.all_gather(lm_head, 'group', axis=1, tiled=True)]
    all_to_all x2 -> x1, waiting for transfers between devices: 28.6 us -> 6.73 us  [from_everyone(): lax.all_to_all(jnp.broadcast_to(array[None], (peers, *array.shape)), axis...]
    all_to_all x1 -> x2, blocking collectives: 14.1 us -> 35.6 us  [from_everyone(): lax.all_to_all(jnp.broadcast_to(array[None], (peers, *array.shape)), axis...]
    all_to_all x2 -> x1, starting transfers between devices: 10.2 us -> 3.32 us  [from_everyone(): lax.all_to_all(jnp.broadcast_to(array[None], (peers, *array.shape)), axis...]
    another operation x0 -> x1, local copies, waits for them, and re-layouts: none -> 5.77 us  [jnp.stack([local for _ in range(lax.axis_size('group'))])]
    all_to_all x0 -> x1, starting transfers between devices: none -> 5.26 us  [lax.all_to_all(jnp.stack([local for _ in range(lax.axis_size('group'))]),...]
  transfers between devices with their start and end apart: 4 -> 3, of which waited for: 4 -> 3; matrix products, arithmetic and copies ran while one was open for 12% -> 1% of each run, Pallas kernels for 0% -> 0%
where the time goes in v1:
time: 450 us; the launch traced here: 449 us
  waiting for transfers between devices  339 us (75%)
  blocking collectives  35.6 us (8%)
  local copies, waits for them, and re-layouts  26.3 us (6%)
  matrix products  17.1 us (4%)
  between operations  14.3 us (3%)
  starting transfers between devices  8.62 us (2%)
  other arithmetic  7.96 us (2%)
    all_to_all x1, waiting for transfers between devices, lax.all_to_all(jnp.stack([local for _ in range(lax.axis_size('group'))]),...  264 us
    all_gather x1, waiting for transfers between devices, sent_together(): result, at, done = (lax.all_gather(both, axis, axis=dim, tiled=True), 0, [])  67.8 us
    all_to_all x2, blocking collectives, from_everyone(): lax.all_to_all(jnp.broadcast_to(array[None], (peers, *array.shape)), axis...  35.6 us
  transfers between devices with their start and end apart: 3, of which 3 were waited for; matrix products, arithmetic and copies ran while one was open for 1% of the time, Pallas kernels for 0%

profile of v1, /device:TPU:0, one launch (start us, length us, event | category | flops | bytes accessed | tf_op | source)
XLA Modules:
  0.0 448.6 jit_solution(14788566867504466074)
XLA Ops:
  7.2 0.0 copy-start.14
  7.2 0.0 copy-start.11
  7.2 0.0 copy-start.15
  7.2 0.0 all-gather.2.cloned.1.call-start
  7.2 0.8 copy.51
  8.1 2.1 concatenate.12
  10.1 0.0 all-gather.2.cloned.1.call-update
  10.2 1.2 exp.69
  11.3 0.8 add.148
  12.1 1.0 fusion.9
  13.1 67.8 %all-gather.2.cloned.1.call-done = bf16[2560,2186]{1,0:T(8,128)(2,1)} async-done(((bf16[160,2186]{1,0:T(8,128)(2,1)}), bf16[2560,2186]{1,0:T(8,128)(2,1)}) %all-gather.2.cloned.1.call-update) | async-done | bytes 11192336 | tf_op jit(solution)/shard_map/all_gather | solution.py:21
  81.0 1.4 slice.210
  82.4 0.0 copy-start.3
  82.4 1.3 fusion.2
  83.7 0.0 copy-done.14
  83.7 0.0 copy-done.11
  83.7 0.0 copy-done.15
  83.7 0.0 copy-done.3
  83.7 0.6 fusion.28
  84.4 6.3 %fusion.26 = (bf16[2560,640]{1,0:T(8,128)(2,1)S(1)}, bf16[2560,640]{1,0:T(8,128)(2,1)}, bf16[2560,640]{1,0:T(8,128)(2,1)S(1)}) fusion(bf16[2560,2186]{1,0:T(8,128)(2,1)} %all-gather.2.cloned.1.call-done), kind=kLoop, calls=%fused_computation.67 | loop fusion | bytes 19660800 | tf_op jit(solution)/shard_map/slice | solution.py:23
  90.7 1.7 copy-done.2
  92.4 0.0 copy-done.4
  92.4 0.0 copy-done.7
  92.4 0.6 fusion.1
  93.0 0.0 copy-done.8
  93.0 0.0 copy-done.12
  93.0 0.1 reduce_sum.103
  93.1 1.4 multiply_exponential_fusion
  94.5 0.1 broadcast_multiply_fusion
  94.6 0.0 copy-start.10
  94.6 4.2 multiply_add_fusion
  98.8 0.0 copy-start
  98.8 0.0 copy-start.16
  98.8 0.0 copy-start.13
  98.8 2.3 copy-done
  101.1 0.0 copy-done.10
  101.1 2.1 fusion.30
  103.3 0.0 copy-done.16
  103.3 0.7 bitcast_add_fusion
  104.0 1.0 reshape.151
  105.0 0.0 copy-done.1
  105.0 0.7 multiply_reduce_fusion.3
  105.7 0.0 copy-start.5
  105.7 14.3 %all_to_all.21 = f32[8,1,16]{2,1,0:T(1,128)S(1)} all-to-all(f32[8,1,16]{2,1,0:T(1,128)S(1)} %broadcast_in_dim.15), channel_id=1, replica_groups=mesh['group'=16,'head'=8] {'head'}, dimensions={0} | all-to-all | bytes 1024 | tf_op jit(solution)/shard_map/all_to_all | solution.py:30
  120.0 0.0 copy-done.13
  120.0 2.9 fusion.15
  122.9 0.1 broadcast_in_dim.16
  123.1 21.3 %all_to_all.22 = f32[8,16,2560]{2,1,0:T(8,128)S(1)} all-to-all(f32[8,16,2560]{2,1,0:T(8,128)S(1)} %broadcast_in_dim.16), channel_id=1, replica_groups=mesh['group'=16,'head'=8] {'head'}, dimensions={0} | all-to-all | bytes 2621440 | tf_op jit(solution)/shard_map/all_to_all | solution.py:30
  144.4 0.0 copy-done.5
  144.4 5.8 %stack.2 = bf16[16,3200,160]{1,2,0:T(8,128)(2,1)} broadcast(bf16[3200,160]{0,1:T(8,128)(2,1)S(1)} %copy-done.5), dimensions={1,2} | broadcast | bytes 17408000 | tf_op jit(solution)/shard_map/stack | solution.py:10
  150.2 5.3 %all-to-all-start.2 = ((bf16[16,3200,160]{1,2,0:T(8,128)(2,1)}), bf16[16,3200,160]{1,2,0:T(8,128)(2,1)}, u32[]{:S(2)}, u32[]{:S(2)}) async-start(bf16[16,3200,160]{1,2,0:T(8,128)(2,1)} %stack.2), calls=%async_computation.2 | async-start | bytes 32768000 | tf_op jit(solution)/shard_map/all_to_all | solution.py:9
  155.5 0.1 reduce_max.28
  155.6 0.1 reduce_sum.107
  155.7 0.1 multiply_reduce_fusion
  155.9 264.1 %all-to-all-done.2 = bf16[16,3200,160]{1,2,0:T(8,128)(2,1)} async-done(((bf16[16,3200,160]{1,2,0:T(8,128)(2,1)}), bf16[16,3200,160]{1,2,0:T(8,128)(2,1)}, u32[]{:S(2)}, u32[]{:S(2)}) %all-to-all-start.2) | async-done | bytes 16384032 | tf_op jit(solution)/shard_map/all_to_all | solution.py:9
  420.0 0.0 copy-done.9
  420.0 8.1 %fusion.29 = (f32[16]{0:T(128)S(1)}, f32[16,3200]{1,0:T(8,128)S(1)}) fusion(bf16[3200,2560]{0,1:T(8,128)(2,1)} %bitcast.7, f32[16,2560]{1,0:T(8,128)S(1)} %reduce_sum.107, bf16[16,2560]{1,0:T(8,128)(2,1)S(1)} %copy-done.4, f32[2560]{0:T(1024)S(1)} %copy-done.9, f32[16]{0:T(128)S(1)} %add_rsqrt_fusion), kind=kOutput, calls=%fused_computation.70 | convolution fusion | flops 262399984 | bytes 16844928 | tf_op jit(solution)/shard_map/dot_general | solution.py:151
  428.1 0.3 select_reduce_fusion
  428.4 0.6 broadcast_in_dim.18
  429.1 3.3 all-to-all-start.3
  432.4 0.9 copy.59
  433.3 6.7 %all-to-all-done.3 = f32[8,6,16]{2,1,0:T(8,128)S(1)} async-done(((f32[8,6,16]{2,1,0:T(8,128)}), f32[8,6,16]{2,1,0:T(8,128)S(1)}, u32[]{:S(2)}, u32[]{:S(2)}) %all-to-all-start.3) | async-done | bytes 3104 | tf_op jit(solution)/shard_map/all_to_all | solution.py:30
  440.7 0.5 subtract_bitcast_fusion
  441.3 0.5 add_bitcast_fusion
  (57 shorter events, 0.8 us)
Async XLA Ops:
  7.2 76.5 %copy-start.14 = (f32[4,256]{1,0:T(4,128)S(1)}, f32[4,256]{1,0:T(4,128)}, u32[]{:S(2)}) copy-start(f32[4,256]{1,0:T(4,128)} %param.36) | copy-start | bytes 12292
  7.2 76.5 %copy-start.11 = (bf16[16,3,256]{2,0,1:T(8,128)(2,1)S(1)}, bf16[16,3,256]{2,0,1:T(8,128)(2,1)}, u32[]{:S(2)}) copy-start(bf16[16,3,256]{2,0,1:T(8,128)(2,1)} %param.25) | copy-start | bytes 73732
  7.2 76.5 %copy-start.15 = (f32[256]{0:T(256)S(1)}, f32[256]{0:T(256)}, u32[]{:S(2)}) copy-start(f32[256]{0:T(256)} %param.37) | copy-start | bytes 3076
  7.2 73.8 %all-gather.2.cloned.1.call-start = ((), (), s32[]{:S(2)}) async-start(), calls=%async_computation.4 | async-start | bytes 12533760 | tf_op jit(solution)/shard_map/all_gather | solution.py:21
  82.4 1.4 copy-start.3
  84.4 8.0 %copy-start.4 = (bf16[16,2560]{1,0:T(8,128)(2,1)S(1)}, bf16[16,2560]{1,0:T(8,128)(2,1)}, u32[]{:S(2)}) copy-start(bf16[16,2560]{1,0:T(8,128)(2,1)} %param.22) | copy-start | bytes 245764
  84.4 8.0 %copy-start.7 = (f32[2560]{0:T(1024)S(1)}, f32[2560]{0:T(1024)}, u32[]{:S(2)}) copy-start(f32[2560]{0:T(1024)} %param.41) | copy-start | bytes 30724
  84.4 8.6 %copy-start.8 = (bf16[16,3,640]{2,0,1:T(8,128)(2,1)S(1)}, bf16[16,3,640]{2,0,1:T(8,128)(2,1)}, u32[]{:S(2)}) copy-start(bf16[16,3,640]{2,0,1:T(8,128)(2,1)} %param.24) | copy-start | bytes 184324
  84.4 8.6 %copy-start.12 = (f32[4,640]{1,0:T(4,128)S(1)}, f32[4,640]{1,0:T(4,128)}, u32[]{:S(2)}) copy-start(f32[4,640]{1,0:T(4,128)} %param.34) | copy-start | bytes 30724
  90.7 1.7 copy-start.2
  90.7 14.3 %copy-start.1 = (bf16[2560,640]{1,0:T(8,128)(2,1)}, bf16[2560,640]{1,0:T(8,128)(2,1)S(1)}, u32[]{:S(2)}) copy-start(bf16[2560,640]{1,0:T(8,128)(2,1)S(1)} %get-tuple-element.62) | copy-start | bytes 9830404
  94.6 6.6 %copy-start.10 = (f32[16,128]{1,0:T(8,128)S(1)}, f32[16,128]{1,0:T(8,128)}, u32[]{:S(2)}) copy-start(f32[16,128]{1,0:T(8,128)} %get-tuple-element.71) | copy-start | bytes 24580
  98.8 2.4 copy-start
  98.8 4.5 copy-start.16
  98.8 21.2 %copy-start.13 = (f32[640]{0:T(1024)S(1)}, f32[640]{0:T(1024)}, u32[]{:S(2)}) copy-start(f32[640]{0:T(1024)} %param.42) | copy-start | bytes 7684
  105.7 38.7 %copy-start.5 = (bf16[3200,160]{0,1:T(8,128)(2,1)S(1)}, bf16[3200,160]{0,1:T(8,128)(2,1)}, u32[]{:S(2)}) copy-start(bf16[3200,160]{0,1:T(8,128)(2,1)} %param.33) | copy-start | bytes 3072004
  150.2 5.3 %copy-start.6 = (bf16[16,3200]{1,0:T(8,128)(2,1)S(1)}, bf16[16,3200]{1,0:T(8,128)(2,1)}, u32[]{:S(2)}) copy-start(bf16[16,3200]{1,0:T(8,128)(2,1)} %param.27) | copy-start | bytes 307204
  150.2 269.8 %copy-start.9 = (f32[2560]{0:T(1024)S(1)}, f32[2560]{0:T(1024)}, u32[]{:S(2)}) copy-start(f32[2560]{0:T(1024)} %param.43) | copy-start | bytes 30724
  150.2 269.8 %all-to-all-start.2 = ((bf16[16,3200,160]{1,2,0:T(8,128)(2,1)}), bf16[16,3200,160]{1,2,0:T(8,128)(2,1)}, u32[]{:S(2)}, u32[]{:S(2)}) async-start(bf16[16,3200,160]{1,2,0:T(8,128)(2,1)} %stack.2), calls=%async_computation.2 | async-start | bytes 32768000 | tf_op jit(solution)/shard_map/all_to_all | solution.py:9
  420.0 8.1 %copy-start.17 = (s32[16]{0:T(128)S(1)}, s32[16]{0:T(128)}, u32[]{:S(2)}) copy-start(s32[16]{0:T(128)} %param.26) | copy-start | bytes 196
  420.0 12.4 %slice-start = ((bf16[2560,2186]{1,0:T(8,128)(2,1)}), bf16[2560,10]{1,0:T(8,128)(2,1)S(1)}, s32[]{:S(2)}) async-start(bf16[2560,2186]{1,0:T(8,128)(2,1)} %all-gather.2.cloned.1.call-done), calls=%async_computation.5 | async-start | bytes 1310720 | tf_op jit(solution)/shard_map/slice | solution.py:23
  429.1 11.0 %all-to-all-start.3 = ((f32[8,6,16]{2,1,0:T(8,128)}), f32[8,6,16]{2,1,0:T(8,128)S(1)}, u32[]{:S(2)}, u32[]{:S(2)}) async-start(f32[8,6,16]{2,1,0:T(8,128)} %broadcast_in_dim.18), calls=%async_computation.3 | async-start | bytes 65536 | tf_op jit(solution)/shard_map/all_to_all | solution.py:30
Sparse Core Ops, SparseCore 0:
  10.3 70.6 all-gather.1
